TPU v7x, 256 devices: a whole 4x4x8 slice. The times are simulated.
256 devices in a mesh: ep: 32 (over x, z_hi, y), dp: 8 (over z_lo, core).
Axes of the slice: x: 4, y: 4, z: 8 (z_hi: 2, z_lo: 4; z = z_hi * 4 + z_lo), core: 2. Of those that a mesh axis runs over, the one named last changes fastest.
Arguments:
- master_weights: float32 [32, 1024, 3584], P('ep', 'dp'), may hold values from -6 to 6
- first_moment: float32 [32, 1024, 3584], P('ep', 'dp'), may hold values from -6 to 6
- second_moment: float32 [32, 1024, 3584], P('ep', 'dp'), may hold values from 0.01 to 4
- expert_ids: int32 [32], replicated, may hold values from 0 to 255, as said below
- bucket_offsets: int32 [1024], replicated, may hold values from 0 to 1023, as said below
- writer_rank: int32 [1024], replicated, may hold values from 0 to 7, as said below
Outputs:
- saved: bfloat16 [3, 32, 1024, 3584], P(None, 'ep', 'dp')
Inputs may be any that keep to these rules, and one draw needn't show every extreme that they name: `expert_ids`: 32 different global expert numbers. `bucket_offsets`: each saved row named exactly once. `writer_rank`: of the bucket rows held by any one dp index, exactly 1024 // (8 * 8) are written by each dp index.
All inputs are finite; a program needn't handle non-finite values.
Results may differ from a plain program's by a relative error of at most 0.001.
Values may be sent and summed in bfloat16 or wider, within the bound.
A program may use at most 128 MiB of HBM per device.

v0:
```python
import functools

import jax
import jax.numpy as jnp
import numpy as np
from jax import lax
from jax.experimental import pallas as pl
from jax.experimental.pallas import tpu as pltpu
from jax.sharding import PartitionSpec as P

MESH = pl.DeviceIdType.MESH
CHUNKS, SUB, WIDTH = 14, 2, 128
BLOCK = 24 * SUB
UNIT = 3 * SUB
BINS = ((0, 2), (3, 5), (6, 6), (7, 7), (8, 8), (9, 9), (10, 10), (11, 12), (13, 16))
XY = (
    (2, 2), (1, 2), (2, 1), (3, 2), (2, 3), (1, 1), (3, 3), (1, 3), (3, 1), (0, 2), (2, 0), (1, 0), (0, 1), (3, 0), (0, 3),
)
LEAD, LAG = 2, 2


def rows_for(n):
    return max(8, -(-UNIT * n // 8) * 8)


def one_hot_rows(slots, rows, start=0):
    at = start + lax.broadcasted_iota(jnp.int32, (rows, slots.shape[1]), 0)
    return jnp.where(at == slots, 1.0, 0.0).astype(jnp.bfloat16)


def fill_one_hot(ref, slots):
    def rows(b, carry):
        first = pl.multiple_of(b * 64, 64)
        ref[pl.ds(first, 64), :] = one_hot_rows(slots, 64, first)
        return carry

    lax.fori_loop(0, ref.shape[0] // 64, rows, 0)


def total_of(mask, value, axis):
    return jnp.sum(jnp.where(mask, value, 0.0), axis=axis, keepdims=True)


def counted(hot):
    earlier = lax.broadcasted_iota(jnp.int32, (128, 128), 0) < lax.broadcasted_iota(jnp.int32, (128, 128), 1)
    ones = jnp.where(hot, 1.0, 0.0).astype(jnp.bfloat16)
    return jnp.dot(ones, jnp.where(earlier, 1.0, 0.0).astype(jnp.bfloat16), preferred_element_type=jnp.float32)


def writers_and_places(writers):
    kind = lax.broadcasted_iota(jnp.int32, (8, 128), 0)
    carry = jnp.zeros((8, 1), jnp.float32)
    within = []
    for a in range(8):
        hot = writers[a : a + 1] == kind
        within.append(total_of(hot, counted(hot) + carry, 0))
        carry = carry + total_of(hot, 1.0, 1)
    return jnp.concatenate([writers.astype(jnp.float32), *within], axis=0).astype(jnp.bfloat16)


def row_facts(known, offsets):
    kind = lax.broadcasted_iota(jnp.int32, (8, 128), 0)
    found = jnp.dot(known, one_hot_rows(offsets % 128, 128), preferred_element_type=jnp.float32)
    row = kind == offsets // 128
    writer, place = total_of(row, found[:8], 0).astype(jnp.int32), total_of(row, found[8:], 0)
    hot = writer == kind
    return writer, place, total_of(hot, counted(hot), 0).astype(jnp.int32)


def landing(known, offsets_ref, dp):
    rows = lax.broadcasted_iota(jnp.int32, (128 * SUB, 128), 0)

    def shard(p, slots):
        writer, place, rank = row_facts(known, offsets_ref[pl.ds(p, 1), :])
        lane = jnp.where(writer == dp, rank * (8 * SUB) + p, -1024)
        hit = lane == rows
        for h in range(1, SUB):
            hit = hit | (lane + 8 * h == rows)
        return slots + lax.dot_general(
            jnp.broadcast_to(place, (8, 128)).astype(jnp.bfloat16), jnp.where(hit, 1.0, 0.0).astype(jnp.bfloat16),
            (((1,), (1,)), ((), ())), preferred_element_type=jnp.float32,
        )

    slots = lax.fori_loop(0, 8, shard, jnp.zeros((8, 128 * SUB), jnp.float32))
    part = (lax.broadcasted_iota(jnp.int32, (1, 128 * SUB), 1) // 8) % SUB
    return slots[0:1].astype(jnp.int32) + part * 128


def comm_kernel(
    same, other, offsets_ref, writers_ref, tab_ref, c2_ref, c3_ref, x0, x1, x2, out,
    xin, sel1, sel2, sel3, sel4, send_a, recv_a, send_s, recv_s, send_o, recv_o, send_b, recv_b,
    in_sem, a_send, a_recv, s_send, s_recv, o_send, o_recv, b_send, b_recv,
):
    ep, dp = lax.axis_index("ep"), lax.axis_index("dp")
    x, zh, y = ep // 8, (ep // 4) % 2, ep % 4
    zl, core = dp // 2, dp % 2
    me = x * 4 + y

    def xy_peer(dx, dy):
        px, py = (x + dx) % 4, (y + dy) % 4
        return px * 4 + py, (px * 8 + zh * 4 + py, dp)

    def dp_peer(dz, dc):
        return ((zl + dz) % 4) * 2 + (core + dc) % 2

    flipped = x * 8 + (1 - zh) * 4 + y
    same_offs = [(a, c) for a in (1, 3, 2) for c in (0, 1)] + [(0, 1)]
    other_offs = [(a, c) for a in (0, 1, 3, 2) for c in (0, 1)]

    barrier = pltpu.get_barrier_semaphore()
    for dx, dy in XY:
        pl.semaphore_signal(barrier, inc=1, device_id=xy_peer(dx, dy)[1], device_id_type=MESH)
    for a, c in same_offs:
        pl.semaphore_signal(barrier, inc=1, device_id=(ep, dp_peer(a, c)), device_id_type=MESH)
    for a, c in other_offs:
        pl.semaphore_signal(barrier, inc=1, device_id=(flipped, dp_peer(a, c)), device_id_type=MESH)

    def load(c, carry):
        cols = pl.ds(pl.multiple_of(c * (SUB * WIDTH), SUB * WIDTH), SUB * WIDTH)
        for f, ref in enumerate((x0, x1, x2)):
            pltpu.make_async_copy(ref.at[:, cols], xin.at[f, c], in_sem.at[f, c]).start()
        return carry

    lax.fori_loop(0, CHUNKS, load, 0)
    known = writers_and_places(writers_ref[...])
    writer, _, rank = row_facts(known, offsets_ref[pl.ds(dp, 1), :])
    slot = rank * (8 * SUB) + writer
    sel1[...] = one_hot_rows(jnp.concatenate([slot + 8 * h for h in range(SUB)], axis=1), 128 * SUB)

    def stage1(c):
        for f in range(3):
            pltpu.make_async_copy(x0.at[:, pl.ds(0, SUB * WIDTH)], xin.at[f, c], in_sem.at[f, c]).wait()
            rows = jnp.concatenate(
                [xin[f, c, :, h * WIDTH : (h + 1) * WIDTH].astype(jnp.bfloat16) for h in range(SUB)], axis=0
            )
            moved = jnp.dot(sel1[...], rows, preferred_element_type=jnp.float32).astype(jnp.bfloat16)
            send_a[c, :, f * 8 * SUB : (f + 1) * 8 * SUB, :] = moved.reshape(16, 8 * SUB, WIDTH)
        recv_a[c, me] = send_a[c, me]

    def start_a(c):
        for dx, dy in XY:
            slot, dev = xy_peer(dx, dy)
            pltpu.make_async_remote_copy(
                send_a.at[c, slot], recv_a.at[c, me], a_send.at[c], a_recv.at[c], device_id=dev, device_id_type=MESH
            ).start()

    peer = xy_peer(1, 0)[1]

    def waiter(src, dst, send, recv):
        return pltpu.make_async_remote_copy(src, dst, send, recv, device_id=peer, device_id_type=MESH)

    def wait_a(c):
        return waiter(send_a.at[c, pl.ds(0, 15)], recv_a.at[c, pl.ds(0, 15)], a_send.at[c], a_recv.at[c])

    def wait_s(c):
        return waiter(send_s.at[c, pl.ds(0, 7)], recv_s.at[c, pl.ds(0, 7)], s_send.at[c], s_recv.at[c])

    def wait_o(c):
        return waiter(send_o.at[c], recv_o.at[c], o_send.at[c], o_recv.at[c])

    def wait_b(c):
        return waiter(send_b.at[c, pl.ds(0, 15)], recv_b.at[c, pl.ds(0, 15)], b_send.at[c], b_recv.at[c])

    def stage2(c):
        wait_a(c).wait_recv()
        rows = recv_a[c].reshape(16 * BLOCK, WIDTH)
        moved = jnp.dot(sel2[...], rows, preferred_element_type=jnp.float32)
        send_o[c] = moved[8 * same :].reshape(8, other // 8, 8, WIDTH).astype(jnp.bfloat16)
        send_s[c] = moved[: 8 * same].reshape(8, same // 8, 8, WIDTH).astype(jnp.bfloat16)
        recv_s[c, dp] = send_s[c, dp]
        for a, k in other_offs:
            to = dp_peer(a, k)
            pltpu.make_async_remote_copy(
                send_o.at[c, to], recv_o.at[c, dp], o_send.at[c], o_recv.at[c], device_id=(flipped, to), device_id_type=MESH
            ).start()
        for a, k in same_offs:
            to = dp_peer(a, k)
            pltpu.make_async_remote_copy(
                send_s.at[c, to], recv_s.at[c, dp], s_send.at[c], s_recv.at[c], device_id=(ep, to), device_id_type=MESH
            ).start()

    def stage3(c):
        wait_o(c).wait_recv()
        wait_s(c).wait_recv()
        rows = jnp.concatenate(
            [
                recv_s[c].astype(jnp.float32).reshape(8 * same, WIDTH),
                recv_o[c].astype(jnp.float32).reshape(8 * other, WIDTH),
            ],
            axis=0,
        ).astype(jnp.bfloat16)
        moved = jnp.dot(sel3[...], rows, preferred_element_type=jnp.float32).astype(jnp.bfloat16)
        send_b[c] = moved.reshape(16, BLOCK, WIDTH)
        recv_b[c, me] = send_b[c, me]
        for dx, dy in XY:
            slot, dev = xy_peer(dx, dy)
            pltpu.make_async_remote_copy(
                send_b.at[c, slot], recv_b.at[c, me], b_send.at[c], b_recv.at[c], device_id=dev, device_id_type=MESH
            ).start()

    def stage4(c):
        wait_b(c).wait_recv()
        for f in range(3):
            rows = recv_b[c, :, f * 8 * SUB : (f + 1) * 8 * SUB, :].reshape(128 * SUB, WIDTH)
            moved = jnp.dot(sel4[...], rows, preferred_element_type=jnp.float32).astype(jnp.bfloat16)
            for h in range(SUB):
                cols = pl.ds(pl.multiple_of((c * SUB + h) * WIDTH, WIDTH), WIDTH)
                out[f, :, cols] = moved[h * 128 : (h + 1) * 128]

    stage1(0)
    pl.semaphore_wait(barrier, len(XY) + len(same_offs) + len(other_offs))
    start_a(0)

    def ahead(c, carry):
        stage1(c)
        start_a(c)
        return carry

    lax.fori_loop(1, LEAD, ahead, 0)
    tab = tab_ref[...].astype(jnp.bfloat16)
    look2 = jnp.dot(tab, one_hot_rows(c2_ref[0:1, :], 128), preferred_element_type=jnp.float32).astype(jnp.int32)
    fill_one_hot(sel2, look2[1:2, :] + jnp.where(look2[2:3, :] > 0, c2_ref[2:3, :], c2_ref[1:2, :]))
    look3 = jnp.dot(tab, one_hot_rows(c3_ref[0:1, :], 128), preferred_element_type=jnp.float32).astype(jnp.int32)
    fill_one_hot(sel3, look3[0:1, :] * BLOCK + c3_ref[1:2, :])
    sel4[...] = one_hot_rows(landing(known, offsets_ref, dp), 128 * SUB)

    def step(s, carry):
        @pl.when(s + LEAD < CHUNKS)
        def _():
            stage1(s + LEAD)
            start_a(s + LEAD)

        @pl.when(s < CHUNKS)
        def _():
            stage2(s)

        @pl.when((s >= LAG) & (s < CHUNKS + LAG))
        def _():
            stage3(s - LAG)

        @pl.when(s >= 2 * LAG)
        def _():
            stage4(s - 2 * LAG)

        return carry

    lax.fori_loop(0, CHUNKS + 2 * LAG, step, 0)

    def finish(c, carry):
        wait_a(c).wait_send()
        wait_s(c).wait_send()
        wait_o(c).wait_send()
        wait_b(c).wait_send()
        return carry

    lax.fori_loop(0, CHUNKS, finish, 0)


def exchange(b, offsets, writers, tab, x0, x1, x2):
    lo, hi = BINS[b]
    other, same = rows_for(hi), rows_for(16 - lo)
    total = 8 * (same + other)
    j, f, h, w = np.meshgrid(np.arange(16), np.arange(3), np.arange(SUB), np.arange(8), indexing="ij")
    j, f, h, w = (v.reshape(-1) for v in (j, f, h, w))
    c2 = np.stack([j, w * same + f * SUB + h, 8 * same + w * other + f * SUB + h])
    r = np.arange(total)
    far = r >= 8 * same
    cap = np.where(far, other, same)
    rr = np.where(far, r - 8 * same, r)
    p, rem = rr // cap, rr % cap
    k, f, h = rem // UNIT, (rem % UNIT) // SUB, rem % SUB
    real = k < 16
    c3 = np.stack([np.where(real, far * 16 + k, 127), np.where(real, f * 8 * SUB + h * 8 + p, -1)])
    vm = pl.BlockSpec(memory_space=pltpu.VMEM)
    hbm = pl.BlockSpec(memory_space=pl.ANY)
    bf = jnp.bfloat16
    blocks = pltpu.VMEM((CHUNKS, 16, BLOCK, WIDTH), bf)
    sems = [pltpu.SemaphoreType.DMA((3, CHUNKS))] + [pltpu.SemaphoreType.DMA((CHUNKS,))] * 8
    return pl.pallas_call(
        functools.partial(comm_kernel, same, other),
        out_shape=jax.ShapeDtypeStruct((3, 128, CHUNKS * SUB * WIDTH), bf),
        in_specs=[vm] * 5 + [hbm] * 3,
        out_specs=vm,
        scratch_shapes=[
            pltpu.VMEM((3, CHUNKS, 128, SUB * WIDTH), jnp.float32),
            pltpu.VMEM((128 * SUB, 128 * SUB), bf),
            pltpu.VMEM((total, 16 * BLOCK), bf),
            pltpu.VMEM((16 * BLOCK, total), bf),
            pltpu.VMEM((128 * SUB, 128 * SUB), bf),
            blocks,
            blocks,
            pltpu.VMEM((CHUNKS, 8, same // 8, 8, WIDTH), bf),
            pltpu.VMEM((CHUNKS, 8, same // 8, 8, WIDTH), bf),
            pltpu.VMEM((CHUNKS, 8, other // 8, 8, WIDTH), bf),
            pltpu.VMEM((CHUNKS, 8, other // 8, 8, WIDTH), bf),
            blocks,
            blocks,
            *sems,
        ],
        compiler_params=pltpu.CompilerParams(
            collective_id=b, has_side_effects=True, vmem_limit_bytes=56 * 1024 * 1024
        ),
        name=f"exchange_{b}",
    )(offsets, writers, tab, jnp.asarray(c2, jnp.int32), jnp.asarray(c3, jnp.int32), x0, x1, x2)


def tables_kernel(ids_ref, which_ref, tab_ref):
    i32, f32 = jnp.int32, jnp.float32
    zh = (lax.axis_index("ep") // 4) % 2

    def at(shape, d):
        return lax.broadcasted_iota(i32, shape, d)

    add = total_of
    eye = at((32, 32), 0) == at((32, 32), 1)

    def col(v):
        return add(eye, v.astype(f32), 1).astype(i32)

    ids, e = ids_ref[...], at((1, 32), 1)
    pos = add(col(ids) < ids, 1.0, 0).astype(i32)
    plane, dz, dxy = (e // 4) % 2, (pos // 4) % 2, (pos // 8) * 4 + pos % 4
    group = (plane * 2 + dz) * 16
    cg, cd = col(group), col(dxy)
    k = add((cg == group) & (cd < dxy), 1.0, 0).astype(i32)
    key = jnp.where(dz == zh, jnp.where(plane == zh, 0, 16) + k, -1)
    lane = at((32, 128), 1)
    dtab = add(col(key) == lane, (cd + 100).astype(f32), 0) - 100.0
    own = (at((32, 128), 0) == (lane // 4) * 8 + zh * 4 + lane % 4) & (lane < 16)
    kj = add(own, (col(k) * UNIT).astype(f32), 0)
    oj = add(own & (col(dz) != zh), 1.0, 0)
    r = at((8, 128), 0)
    tab_ref[...] = jnp.where(r == 0, dtab, jnp.where(r == 1, kj, jnp.where(r == 2, oj, 0.0)))
    m = jnp.sum(jnp.where((plane == 0) & (dz == 1), 1.0, 0.0)).astype(i32)
    which = jnp.int32(0)
    for _, hi in BINS[:-1]:
        which = which + jnp.where(m > hi, 1, 0)
    which_ref[0, 0] = which


def tables(expert_ids):
    vm = pl.BlockSpec(memory_space=pltpu.VMEM)
    return pl.pallas_call(
        tables_kernel,
        out_shape=(jax.ShapeDtypeStruct((1, 1), jnp.int32), jax.ShapeDtypeStruct((8, 128), jnp.float32)),
        in_specs=[vm],
        out_specs=(pl.BlockSpec(memory_space=pltpu.SMEM), vm),
        name="tables",
    )(expert_ids.reshape(1, 32))


def on_device(master_weights, first_moment, second_moment, expert_ids, bucket_offsets, writer_rank):
    which, tab = tables(expert_ids)
    saved = lax.switch(
        which[0, 0],
        [functools.partial(exchange, b) for b in range(len(BINS))],
        bucket_offsets.reshape(8, 128), writer_rank.reshape(8, 128), tab, master_weights[0], first_moment[0], second_moment[0],
    )
    return saved[:, None]


def solution(mesh):
    return jax.shard_map(
        on_device,
        mesh=mesh,
        in_specs=(P("ep", "dp", None), P("ep", "dp", None), P("ep", "dp", None), P(), P(), P()),
        out_specs=P(None, "ep", "dp", None),
        check_vma=False,
    )
```

profile of v0, /device:TPU:1, one launch (start us, length us, event | category | flops | bytes accessed | tf_op | source)
XLA Modules:
  0.0 112.4 jit_solution(15860931284797794592)
XLA Ops:
  0.0 1.4 %tables.1 = (s32[1,1]{1,0:T(1,128)}, f32[8,128]{1,0:T(8,128)S(1)}) custom-call(s32[1,32]{1,0:T(1,128)} %bitcast.88), custom_call_target="tpu_custom_call" | custom-call | tf_op jit(solution)/shard_map/tables/pallas_call | solution.py:343
  2.1 108.8 %conditional.1 = (bf16[3,1,128,3584]{3,2,1,0:T(8,128)(2,1)S(1)}) conditional(s32[]{:T(128)} %bitcast.1, (s32[8,128]{1,0:T(8,128)}, s32[8,128]{1,0:T(8,128)}, f32[8,128]{1,0:T(8,128)S(1)}, f32[128,3584]{1,0:T(8,128)}, f32[128,3584]{1,0:T(8,128)}, /*index=5*/f32[128,3584]{1,0:T(8,128)}) %tuple.158, ...), branch_computations={%region_0.0_spmd.clone, %region_1.0_spmd.clone, %region_2.0_spmd.c... | conditional | bytes 8 | solution.py:354
  2.3 108.3 %exchange_6.1 = bf16[3,128,3584]{2,1,0:T(8,128)(2,1)S(1)} custom-call(s32[8,128]{1,0:T(8,128)} %get-tuple-element.345.offsets_ref, s32[8,128]{1,0:T(8,128)} %get-tuple-element.346.writers_ref, f32[8,128]{1,0:T(8,128)S(1)} %get-tuple-element.347.tab_ref, s32[3,768]{1,0:T(4,128)} %constant.54.clone.2.c2_ref, s32[2,832]{1,0:T(2,128)} %constant.55.clone.2.c3_ref, ...), custom_call_target="tpu_custom_call" | custom-call | tf_op jit(solution)/shard_map/cond/branch_6_fun/exchange_6/pallas_call | solution.py:279
  110.9 1.5 %copy.99 = bf16[3,1,128,3584]{3,2,1,0:T(8,128)(2,1)} copy(bf16[3,1,128,3584]{3,2,1,0:T(8,128)(2,1)S(1)} %get-tuple-element.381) | data formatting | bytes 5505024
where the time goes:
time: 113 us; the launch traced here: 112 us
  Pallas kernels  110 us (97%)
  local copies, waits for them, and re-layouts  1.54 us (1%)
    pallas_call x1, Pallas kernels, exchange(): pl.pallas_call(functools.partial(comm_kernel, same, other), out_shape=jax...  108 us

commit v1 on v0

--- a/solution.py
+++ b/solution.py
@@ -16,6 +16,7 @@
 XY = (
     (2, 2), (1, 2), (2, 1), (3, 2), (2, 3), (1, 1), (3, 3), (1, 3), (3, 1), (0, 2), (2, 0), (1, 0), (0, 1), (3, 0), (0, 3),
 )
+ZC = tuple((1, a, c) for a in (0, 1, 3, 2) for c in (0, 1)) + tuple((0, a, c) for a in (1, 3, 2) for c in (0, 1)) + ((0, 0, 1),)
 LEAD, LAG = 2, 2
 
 
@@ -41,54 +42,58 @@
     return jnp.sum(jnp.where(mask, value, 0.0), axis=axis, keepdims=True)
 
 
+def side_by_side(v):
+    return jnp.concatenate([v[8 * a : 8 * (a + 1)] for a in range(8)], axis=1)
+
+
 def counted(hot):
     earlier = lax.broadcasted_iota(jnp.int32, (128, 128), 0) < lax.broadcasted_iota(jnp.int32, (128, 128), 1)
-    ones = jnp.where(hot, 1.0, 0.0).astype(jnp.bfloat16)
-    return jnp.dot(ones, jnp.where(earlier, 1.0, 0.0).astype(jnp.bfloat16), preferred_element_type=jnp.float32)
-
-
-def writers_and_places(writers):
-    kind = lax.broadcasted_iota(jnp.int32, (8, 128), 0)
+    ones = jnp.where(hot, 1.0, 0.0)
+    ones = jnp.concatenate([ones[:, 128 * a : 128 * (a + 1)] for a in range(8)], axis=0).astype(jnp.bfloat16)
+    return side_by_side(jnp.dot(ones, jnp.where(earlier, 1.0, 0.0).astype(jnp.bfloat16), preferred_element_type=jnp.float32))
+
+
+def in_lanes(v):
+    return jnp.concatenate([v[a : a + 1] for a in range(8)], axis=1)
+
+
+def row_facts(writers, offsets):
+    kind = lax.broadcasted_iota(jnp.int32, (8, 1024), 0)
+    hot = in_lanes(writers) == kind
+    count = counted(hot)
     carry = jnp.zeros((8, 1), jnp.float32)
     within = []
     for a in range(8):
-        hot = writers[a : a + 1] == kind
-        within.append(total_of(hot, counted(hot) + carry, 0))
-        carry = carry + total_of(hot, 1.0, 1)
-    return jnp.concatenate([writers.astype(jnp.float32), *within], axis=0).astype(jnp.bfloat16)
-
-
-def row_facts(known, offsets):
-    kind = lax.broadcasted_iota(jnp.int32, (8, 128), 0)
-    found = jnp.dot(known, one_hot_rows(offsets % 128, 128), preferred_element_type=jnp.float32)
-    row = kind == offsets // 128
+        here = slice(128 * a, 128 * (a + 1))
+        within.append(total_of(hot[:, here], count[:, here] + carry, 0))
+        carry = carry + total_of(hot[:, here], 1.0, 1)
+    known = jnp.concatenate([writers.astype(jnp.float32), *within], axis=0).astype(jnp.bfloat16)
+    lanes = in_lanes(offsets)
+    found = jnp.dot(known, one_hot_rows(lanes % 128, 128), preferred_element_type=jnp.float32)
+    row = kind == lanes // 128
     writer, place = total_of(row, found[:8], 0).astype(jnp.int32), total_of(row, found[8:], 0)
     hot = writer == kind
     return writer, place, total_of(hot, counted(hot), 0).astype(jnp.int32)
 
 
-def landing(known, offsets_ref, dp):
-    rows = lax.broadcasted_iota(jnp.int32, (128 * SUB, 128), 0)
-
-    def shard(p, slots):
-        writer, place, rank = row_facts(known, offsets_ref[pl.ds(p, 1), :])
-        lane = jnp.where(writer == dp, rank * (8 * SUB) + p, -1024)
-        hit = lane == rows
-        for h in range(1, SUB):
-            hit = hit | (lane + 8 * h == rows)
-        return slots + lax.dot_general(
-            jnp.broadcast_to(place, (8, 128)).astype(jnp.bfloat16), jnp.where(hit, 1.0, 0.0).astype(jnp.bfloat16),
-            (((1,), (1,)), ((), ())), preferred_element_type=jnp.float32,
-        )
-
-    slots = lax.fori_loop(0, 8, shard, jnp.zeros((8, 128 * SUB), jnp.float32))
+def landing(writer, place, rank, dp):
+    shard = lax.broadcasted_iota(jnp.int32, (1, 1024), 1) // 128
+    rows = lax.broadcasted_iota(jnp.int32, (128 * SUB, 1024), 0)
+    lane = jnp.where(writer == dp, rank * (8 * SUB) + shard, -1024)
+    hit = lane == rows
+    for h in range(1, SUB):
+        hit = hit | (lane + 8 * h == rows)
+    slots = lax.dot_general(
+        jnp.broadcast_to(place, (8, 1024)).astype(jnp.bfloat16), jnp.where(hit, 1.0, 0.0).astype(jnp.bfloat16),
+        (((1,), (1,)), ((), ())), preferred_element_type=jnp.float32,
+    )
     part = (lax.broadcasted_iota(jnp.int32, (1, 128 * SUB), 1) // 8) % SUB
     return slots[0:1].astype(jnp.int32) + part * 128
 
 
 def comm_kernel(
     same, other, offsets_ref, writers_ref, tab_ref, c2_ref, c3_ref, x0, x1, x2, out,
-    xin, sel1, sel2, sel3, sel4, send_a, recv_a, send_s, recv_s, send_o, recv_o, send_b, recv_b,
+    held, xin, sel1, sel2, sel3, sel4, send_a, recv_a, send_s, recv_s, send_o, recv_o, send_b, recv_b,
     in_sem, a_send, a_recv, s_send, s_recv, o_send, o_recv, b_send, b_recv,
 ):
     ep, dp = lax.axis_index("ep"), lax.axis_index("dp")
@@ -104,8 +109,8 @@
         return ((zl + dz) % 4) * 2 + (core + dc) % 2
 
     flipped = x * 8 + (1 - zh) * 4 + y
-    same_offs = [(a, c) for a in (1, 3, 2) for c in (0, 1)] + [(0, 1)]
-    other_offs = [(a, c) for a in (0, 1, 3, 2) for c in (0, 1)]
+    same_offs = [(a, c) for far, a, c in ZC if not far]
+    other_offs = [(a, c) for far, a, c in ZC if far]
 
     barrier = pltpu.get_barrier_semaphore()
     for dx, dy in XY:
@@ -122,9 +127,10 @@
         return carry
 
     lax.fori_loop(0, CHUNKS, load, 0)
-    known = writers_and_places(writers_ref[...])
-    writer, _, rank = row_facts(known, offsets_ref[pl.ds(dp, 1), :])
-    slot = rank * (8 * SUB) + writer
+    writer, place, rank = row_facts(writers_ref[...], offsets_ref[...])
+    for p in range(8):
+        held[p : p + 1, :] = (rank * (8 * SUB) + writer)[:, 128 * p : 128 * (p + 1)]
+    slot = held[pl.ds(dp, 1), :]
     sel1[...] = one_hot_rows(jnp.concatenate([slot + 8 * h for h in range(SUB)], axis=1), 128 * SUB)
 
     def stage1(c):
@@ -168,15 +174,14 @@
         send_o[c] = moved[8 * same :].reshape(8, other // 8, 8, WIDTH).astype(jnp.bfloat16)
         send_s[c] = moved[: 8 * same].reshape(8, same // 8, 8, WIDTH).astype(jnp.bfloat16)
         recv_s[c, dp] = send_s[c, dp]
-        for a, k in other_offs:
+        for far, a, k in ZC:
             to = dp_peer(a, k)
+            if far:
+                src, dst, sems, at = send_o, recv_o, (o_send.at[c], o_recv.at[c]), flipped
+            else:
+                src, dst, sems, at = send_s, recv_s, (s_send.at[c], s_recv.at[c]), ep
             pltpu.make_async_remote_copy(
-                send_o.at[c, to], recv_o.at[c, dp], o_send.at[c], o_recv.at[c], device_id=(flipped, to), device_id_type=MESH
-            ).start()
-        for a, k in same_offs:
-            to = dp_peer(a, k)
-            pltpu.make_async_remote_copy(
-                send_s.at[c, to], recv_s.at[c, dp], s_send.at[c], s_recv.at[c], device_id=(ep, to), device_id_type=MESH
+                src.at[c, to], dst.at[c, dp], *sems, device_id=(at, to), device_id_type=MESH
             ).start()
 
     def stage3(c):
@@ -199,6 +204,9 @@
             ).start()
 
     def stage4(c):
+        wait_a(c).wait_send()
+        wait_s(c).wait_send()
+        wait_o(c).wait_send()
         wait_b(c).wait_recv()
         for f in range(3):
             rows = recv_b[c, :, f * 8 * SUB : (f + 1) * 8 * SUB, :].reshape(128 * SUB, WIDTH)
@@ -211,18 +219,21 @@
     pl.semaphore_wait(barrier, len(XY) + len(same_offs) + len(other_offs))
     start_a(0)
 
+    tab = tab_ref[...].astype(jnp.bfloat16)
+    look2 = jnp.dot(tab, one_hot_rows(c2_ref[0:1, :], 128), preferred_element_type=jnp.float32).astype(jnp.int32)
+    fill_one_hot(sel2, look2[1:2, :] + jnp.where(look2[2:3, :] > 0, c2_ref[2:3, :], c2_ref[1:2, :]))
+
+    sel4[...] = one_hot_rows(landing(writer, place, rank, dp), 128 * SUB)
+
     def ahead(c, carry):
         stage1(c)
         start_a(c)
         return carry
 
     lax.fori_loop(1, LEAD, ahead, 0)
-    tab = tab_ref[...].astype(jnp.bfloat16)
-    look2 = jnp.dot(tab, one_hot_rows(c2_ref[0:1, :], 128), preferred_element_type=jnp.float32).astype(jnp.int32)
-    fill_one_hot(sel2, look2[1:2, :] + jnp.where(look2[2:3, :] > 0, c2_ref[2:3, :], c2_ref[1:2, :]))
-    look3 = jnp.dot(tab, one_hot_rows(c3_ref[0:1, :], 128), preferred_element_type=jnp.float32).astype(jnp.int32)
-    fill_one_hot(sel3, look3[0:1, :] * BLOCK + c3_ref[1:2, :])
-    sel4[...] = one_hot_rows(landing(known, offsets_ref, dp), 128 * SUB)
+    def late_tables():
+        look3 = jnp.dot(tab, one_hot_rows(c3_ref[0:1, :], 128), preferred_element_type=jnp.float32).astype(jnp.int32)
+        fill_one_hot(sel3, look3[0:1, :] * BLOCK + c3_ref[1:2, :])
 
     def step(s, carry):
         @pl.when(s + LEAD < CHUNKS)
@@ -234,6 +245,8 @@
         def _():
             stage2(s)
 
+        pl.when(s == 1)(late_tables)
+
         @pl.when((s >= LAG) & (s < CHUNKS + LAG))
         def _():
             stage3(s - LAG)
@@ -247,9 +260,6 @@
     lax.fori_loop(0, CHUNKS + 2 * LAG, step, 0)
 
     def finish(c, carry):
-        wait_a(c).wait_send()
-        wait_s(c).wait_send()
-        wait_o(c).wait_send()
         wait_b(c).wait_send()
         return carry
 
@@ -282,6 +292,7 @@
         in_specs=[vm] * 5 + [hbm] * 3,
         out_specs=vm,
         scratch_shapes=[
+            pltpu.VMEM((8, 128), jnp.int32),
             pltpu.VMEM((3, CHUNKS, 128, SUB * WIDTH), jnp.float32),
             pltpu.VMEM((128 * SUB, 128 * SUB), bf),
             pltpu.VMEM((total, 16 * BLOCK), bf),

time: 113 us -> 93.9 us (0.83)
  Pallas kernels: 110 us -> 90.8 us
    pallas_call x1, Pallas kernels: 108 us -> 89.4 us  [exchange(): pl.pallas_call(functools.partial(comm_kernel, same, other), out_shape=jax...]
where the time goes in v1:
time: 93.9 us; the launch traced here: 93.8 us
  Pallas kernels  90.8 us (97%)
  local copies, waits for them, and re-layouts  1.54 us (2%)
    pallas_call x1, Pallas kernels, exchange(): pl.pallas_call(functools.partial(comm_kernel, same, other), out_shape=jax...  89.4 us

profile of v1, /device:TPU:1, one launch (start us, length us, event | category | flops | bytes accessed | tf_op | source)
XLA Modules:
  0.0 93.8 jit_solution(14229219764073886541)
XLA Ops:
  0.0 1.4 %tables.1 = (s32[1,1]{1,0:T(1,128)}, f32[8,128]{1,0:T(8,128)S(1)}) custom-call(s32[1,32]{1,0:T(1,128)} %bitcast.88), custom_call_target="tpu_custom_call" | custom-call | tf_op jit(solution)/shard_map/tables/pallas_call | solution.py:354
  2.1 90.2 %conditional.1 = (bf16[3,1,128,3584]{3,2,1,0:T(8,128)(2,1)S(1)}) conditional(s32[]{:T(128)} %bitcast.1, (s32[8,128]{1,0:T(8,128)}, s32[8,128]{1,0:T(8,128)}, f32[8,128]{1,0:T(8,128)S(1)}, f32[128,3584]{1,0:T(8,128)}, f32[128,3584]{1,0:T(8,128)}, /*index=5*/f32[128,3584]{1,0:T(8,128)}) %tuple.158, ...), branch_computations={%region_0.0_spmd.clone, %region_1.0_spmd.clone, %region_2.0_spmd.c... | conditional | bytes 8 | solution.py:365
  2.3 89.4 %exchange_3.1 = bf16[3,128,3584]{2,1,0:T(8,128)(2,1)S(1)} custom-call(s32[8,128]{1,0:T(8,128)} %get-tuple-element.309.offsets_ref, s32[8,128]{1,0:T(8,128)} %get-tuple-element.310.writers_ref, f32[8,128]{1,0:T(8,128)S(1)} %get-tuple-element.311.tab_ref, s32[3,768]{1,0:T(4,128)} %constant.48.clone.2.c2_ref, s32[2,832]{1,0:T(2,128)} %constant.49.clone.2.c3_ref, ...), custom_call_target="tpu_custom_call" | custom-call | tf_op jit(solution)/shard_map/cond/branch_3_fun/exchange_3/pallas_call | solution.py:289
  92.3 1.5 %copy.99 = bf16[3,1,128,3584]{3,2,1,0:T(8,128)(2,1)} copy(bf16[3,1,128,3584]{3,2,1,0:T(8,128)(2,1)S(1)} %get-tuple-element.381) | data formatting | bytes 5505024
